TPU v7x, 32 devices: a whole 2x2x4 slice. The times are simulated.
32 devices in a mesh: len: 2 (over x), tile: 16 (over z, y, core).
Axes of the slice: x: 2, y: 2, z: 4, core: 2. Of those that a mesh axis runs over, the one named last changes fastest.
Arguments:
- series: float32 [9216], P('tile'), may hold values from -24 to 24
- window_lengths: int32 [4], P('len'), may hold values from 64 to 1024, as said below
- exclusion: int32 [4], P('len'), may hold values from 16 to 256
- tile_list: int32 [64, 2], P('tile'), may hold values from 0 to 15, as said below
Outputs:
- right_profile: float32 [4, 8192], P(None, 'tile')
- left_profile: float32 [4, 8192], P(None, 'tile')
Inputs may be any that keep to these rules, and one draw needn't show every extreme that they name: `window_lengths`: the largest is exactly 1024. `tile_list`: each row is a pair (row block, column block) with row block <= column block; no pair appears twice.
All inputs are finite; a program needn't handle non-finite values.
Results may differ from a plain program's by a relative error of at most 0.00039.
Values sent between devices are 32-bit elements; how exact they have to be, the bound alone decides.
A program may use at most 64 MiB of HBM per device.

v0:
```python
import jax
import jax.numpy as jnp
from jax import lax
from jax.sharding import PartitionSpec as P

MAX_LEN = 1024
TILE_SIDE = 512
COL_BLOCK = 512


EMPTY_VALUE = 2.0
VAR_EPS = 1e-05


def shifted_block(segment, offset, columns, positions):
    window = lax.dynamic_slice_in_dim(segment, offset, positions + columns)
    stride = positions + columns + 1
    repeated = jnp.tile(window, columns + 1)[: columns * stride]
    return repeated.reshape(columns, stride)[:, :positions]


def window_stats(segment, length, positions, columns):
    blocks = (length + columns - 1) // columns
    col_ids = lax.broadcasted_iota(jnp.int32, (columns, 1), 0)
    denominator = length.astype(jnp.float32)
    initial = jnp.zeros((positions,), jnp.float32)

    def add_sum(part_index, running):
        values = shifted_block(segment, part_index * columns, columns, positions)
        inside = col_ids + part_index * columns < length
        return running + jnp.sum(jnp.where(inside, values, 0.0), axis=0)

    centre = lax.fori_loop(0, blocks, add_sum, initial) / denominator

    def add_square(part_index, running):
        values = shifted_block(segment, part_index * columns, columns, positions) - centre[None, :]
        inside = col_ids + part_index * columns < length
        return running + jnp.sum(jnp.where(inside, values * values, 0.0), axis=0)

    spread = lax.fori_loop(0, blocks, add_square, initial) / denominator
    return (centre, 1.0 / jnp.sqrt(spread + VAR_EPS))


def normalized(segment, part_index, centre, inverse, length):
    values = shifted_block(segment, part_index * COL_BLOCK, COL_BLOCK, TILE_SIDE)
    col_ids = lax.broadcasted_iota(jnp.int32, (COL_BLOCK, 1), 0)
    inside = col_ids + part_index * COL_BLOCK < length
    return jnp.where(inside, (values - centre[None, :]) * inverse[None, :], 0.0).astype(
        jnp.bfloat16
    )


def tile_minima(
    row_segment, col_segment, row_stats, col_stats, length, barrier, row_start, col_start, active
):
    blocks = jnp.where(active, (length + COL_BLOCK - 1) // COL_BLOCK, 0)

    def add_block(part_index, running):
        row_normal = normalized(row_segment, part_index, row_stats[0], row_stats[1], length)
        col_normal = normalized(col_segment, part_index, col_stats[0], col_stats[1], length)
        return running + lax.dot_general(
            row_normal, col_normal, (((0,), (0,)), ((), ())), preferred_element_type=jnp.float32
        )

    product = lax.fori_loop(0, blocks, add_block, jnp.zeros((TILE_SIDE, TILE_SIDE), jnp.float32))
    distance = 1.0 - product / length.astype(jnp.float32)
    row_ids = row_start + lax.broadcasted_iota(jnp.int32, (TILE_SIDE, 1), 0)
    col_ids = col_start + lax.broadcasted_iota(jnp.int32, (1, TILE_SIDE), 1)
    allowed = jnp.logical_and(col_ids - row_ids > barrier, active)
    distance = jnp.where(allowed, distance, EMPTY_VALUE)
    return (jnp.min(distance, axis=1), jnp.min(distance, axis=0))


def shared_stats(full_series, lengths):
    time_share = (full_series.shape[0] - MAX_LEN) // lax.axis_size("tile")
    segment = lax.dynamic_slice_in_dim(
        full_series, lax.axis_index("tile") * time_share, time_share + MAX_LEN
    )

    def one_length(length):
        return window_stats(segment, length, time_share, COL_BLOCK)

    centres, inverses = lax.map(one_length, lengths)
    return (
        lax.all_gather(centres, "tile", axis=1, tiled=True),
        lax.all_gather(inverses, "tile", axis=1, tiled=True),
    )


def sweep(full_series, lengths, barriers, tile_slots, alive_slots, stats_all):
    count_len = lengths.shape[0]
    positions = full_series.shape[0] - MAX_LEN
    blank = jnp.full((count_len, positions), EMPTY_VALUE, jnp.float32)

    def per_slot(slot_index, profiles):
        row_start = tile_slots[slot_index, 0] * TILE_SIDE
        col_start = tile_slots[slot_index, 1] * TILE_SIDE
        active = alive_slots[slot_index]
        row_segment = lax.dynamic_slice_in_dim(full_series, row_start, TILE_SIDE + MAX_LEN)
        col_segment = lax.dynamic_slice_in_dim(full_series, col_start, TILE_SIDE + MAX_LEN)

        def per_length(length_index, current):
            right_lowest_distance, left_best = current
            length = lengths[length_index]
            barrier = barriers[length_index]
            row_stats = tuple(
                (
                    lax.dynamic_slice(source, (length_index, row_start), (1, TILE_SIDE))[0]
                    for source in stats_all
                )
            )
            col_stats = tuple(
                (
                    lax.dynamic_slice(source, (length_index, col_start), (1, TILE_SIDE))[0]
                    for source in stats_all
                )
            )
            right_min, left_min = tile_minima(
                row_segment,
                col_segment,
                row_stats,
                col_stats,
                length,
                barrier,
                row_start,
                col_start,
                active,
            )
            right_old = lax.dynamic_slice(
                right_lowest_distance, (length_index, row_start), (1, TILE_SIDE)
            )
            right_lowest_distance = lax.dynamic_update_slice(
                right_lowest_distance,
                jnp.minimum(right_old, right_min[None, :]),
                (length_index, row_start),
            )
            left_old = lax.dynamic_slice(left_best, (length_index, col_start), (1, TILE_SIDE))
            left_best = lax.dynamic_update_slice(
                left_best, jnp.minimum(left_old, left_min[None, :]), (length_index, col_start)
            )
            return (right_lowest_distance, left_best)

        return lax.fori_loop(0, count_len, per_length, profiles)

    return lax.fori_loop(0, tile_slots.shape[0], per_slot, (blank, blank))


def merge_tile(right_lowest_distance, left_best):
    count_tile = lax.axis_size("tile")
    rows_len, positions = right_lowest_distance.shape
    time_share = positions // count_tile
    right_parts, left_parts = (
        lax.all_to_all(
            right_lowest_distance.reshape(rows_len, count_tile, time_share),
            "tile",
            split_axis=1,
            concat_axis=1,
            tiled=True,
        ),
        lax.all_to_all(
            left_best.reshape(rows_len, count_tile, time_share),
            "tile",
            split_axis=1,
            concat_axis=1,
            tiled=True,
        ),
    )
    merged = (jnp.min(right_parts, axis=1), jnp.min(left_parts, axis=1))
    return merged


def shards(series, window_lengths, exclusion, tile_list):
    full_series = lax.all_gather(series, "tile", axis=0, tiled=True)
    lengths, barriers = (window_lengths, exclusion)
    alive_slots = jnp.ones((tile_list.shape[0],), jnp.bool_)
    stats_all = shared_stats(full_series, lengths)
    right_lowest_distance, left_best = sweep(
        full_series, lengths, barriers, tile_list, alive_slots, stats_all
    )
    right_lowest_distance, left_best = merge_tile(right_lowest_distance, left_best)
    right_lowest_distance, left_best = (
        lax.all_gather(right_lowest_distance, "len", axis=0, tiled=True),
        lax.all_gather(left_best, "len", axis=0, tiled=True),
    )
    return (right_lowest_distance, left_best)


def solution(mesh):
    return jax.shard_map(
        shards,
        mesh=mesh,
        in_specs=(P("tile"), P("len"), P("len"), P("tile", None)),
        out_specs=(P(None, "tile"), P(None, "tile")),
        check_vma=False,
    )
```

profile of v0, /device:TPU:0, one launch (start us, length us, event | category | flops | bytes accessed | tf_op | source)
XLA Modules:
  0.0 429.8 jit_solution(2934008944856751509)
XLA Ops:
  3.5 63.0 %all-reduce = f32[9216]{0:T(1024)S(1)} all-reduce(f32[9216]{0:T(1024)S(1)} %dynamic-update-slice), channel_id=1, replica_groups=mesh['len'=2,'tile'=16] {'tile'}, use_global_device_ids=true, to_apply=%add | all-reduce | flops 9216 | bytes 73728
  67.0 41.6 %while.171 = (s32[]{:T(128)}, f32[2,512]{1,0:T(2,128)S(1)}, f32[2,512]{1,0:T(2,128)S(1)}, s32[2]{0:T(128)}, f32[1536]{0:T(1024)S(1)}, /*index=5*/s32[]{:T(128)},...) while((s32[]{:T(128)}, f32[2,512]{1,0:T(2,128)S(1)}, ...), condition=%wide.region_7.8_spmd, body=%wide.region_0.7_spmd.sunk | while | flops 1576479 | bytes 23167832 | solution.py:83
  69.0 6.0 %while.174 = (s32[]{:T(128)}, f32[512]{0:T(512)S(1)}, s32[]{:T(128)}, s32[]{:T(128)}, f32[1536]{0:T(1024)S(1)}, /*index=5*/s32[]{:T(128)}, s32[]{:T(128)}, s32[]{:T(128)}, s32[]{:T(128)}) while((s32[]{:T(128)}, f32[512]{0:T(512)S(1)}, s32[]{:T(128)}, s32[]{:T(128)}, f32[1536]{0:T(1024)S(1)}, /*index=5*/s32[]{:T(128)}, s32[]{:T(128)}, ...), condition=%wide.region_3.3_spmd.clone, body=%wide.region_1.2_spmd.clone.sunk | while | flops 525318 | bytes 11572375 | solution.py:33
  75.6 6.0 %while.175 = (s32[]{:T(128)}, f32[512]{0:T(512)S(1)}, s32[]{:T(128)}, s32[]{:T(128)}, f32[1536]{0:T(1024)S(1)}, /*index=5*/f32[512]{0:T(512)S(1)}, s32[]{:T(128)}, s32[]{:T(128)}, s32[]{:T(128)}, s32[]{:T(128)}) while((s32[]{:T(128)}, f32[512]{0:T(512)S(1)}, s32[]{:T(128)}, s32[]{:T(128)}, f32[1536]{0:T(1024)S(1)}, ...), condition=%wide.region_6.6_spmd.clone, body=%wide.region_4.5_spmd.clone.sunk | while | flops 1049606 | bytes 11574431 | solution.py:40
  83.7 12.1 %while.174 = (s32[]{:T(128)}, f32[512]{0:T(512)S(1)}, s32[]{:T(128)}, s32[]{:T(128)}, f32[1536]{0:T(1024)S(1)}, /*index=5*/s32[]{:T(128)}, s32[]{:T(128)}, s32[]{:T(128)}, s32[]{:T(128)}) while((s32[]{:T(128)}, f32[512]{0:T(512)S(1)}, s32[]{:T(128)}, s32[]{:T(128)}, f32[1536]{0:T(1024)S(1)}, /*index=5*/s32[]{:T(128)}, s32[]{:T(128)}, ...), condition=%wide.region_3.3_spmd.clone, body=%wide.region_1.2_spmd.clone.sunk | while | flops 525318 | bytes 11572375 | solution.py:33
  96.4 12.1 %while.175 = (s32[]{:T(128)}, f32[512]{0:T(512)S(1)}, s32[]{:T(128)}, s32[]{:T(128)}, f32[1536]{0:T(1024)S(1)}, /*index=5*/f32[512]{0:T(512)S(1)}, s32[]{:T(128)}, s32[]{:T(128)}, s32[]{:T(128)}, s32[]{:T(128)}) while((s32[]{:T(128)}, f32[512]{0:T(512)S(1)}, s32[]{:T(128)}, s32[]{:T(128)}, f32[1536]{0:T(1024)S(1)}, ...), condition=%wide.region_6.6_spmd.clone, body=%wide.region_4.5_spmd.clone.sunk | while | flops 1049606 | bytes 11574431 | solution.py:40
  108.6 17.3 %all_gather.16 = f32[2,8192]{1,0:T(2,128)S(1)} all-gather(f32[2,512]{1,0:T(2,128)S(1)} %get-tuple-element.1002), channel_id=1, replica_groups=mesh['len'=2,'tile'=16] {'tile'}, dimensions={1}, use_global_device_ids=true | all-gather | bytes 69632 | tf_op jit(solution)/shard_map/all_gather | solution.py:85
  125.9 20.6 %all_gather.17 = f32[2,8192]{1,0:T(2,128)} all-gather(f32[2,512]{1,0:T(2,128)S(1)} %get-tuple-element.1003), channel_id=1, replica_groups=mesh['len'=2,'tile'=16] {'tile'}, dimensions={1}, use_global_device_ids=true | all-gather | bytes 69632 | tf_op jit(solution)/shard_map/all_gather | solution.py:86
  147.8 256.3 %while.173 = (s32[]{:T(128)}, f32[2,8192]{1,0:T(2,128)}, f32[2,8192]{1,0:T(2,128)}, s32[4,2]{0,1:T(2,128)}, f32[9216]{0:T(1024)}, /*index=5*/s32[2]{0:T(128)}, s...) while((s32[]{:T(128)}, f32[2,8192]{1,0:T(2,128)}, ...), condition=%wide.region_15.16_spmd, body=%wide.region_8.15_spmd.sunk | while | flops 272631840 | bytes 27405192 | solution.py:145
  151.4 60.5 %while.176 = (s32[]{:T(128)}, f32[2,8192]{1,0:T(2,128)}, f32[2,8192]{1,0:T(2,128)}, s32[]{:T(128)}, s32[]{:T(128)}, /*index=5*/s32[]{:T(128)}, s32[2]{0:T(128)},...) while((s32[]{:T(128)}, f32[2,8192]{1,0:T(2,128)}, ...), condition=%wide.region_14.14_spmd, body=%wide.region_9.13_spmd.sunk | while | flops 272631840 | bytes 27380040 | solution.py:143
  154.3 14.3 %while.177 = (s32[]{:T(128)}, f32[512,512]{1,0:T(8,128)S(1)}, s32[]{:T(128)}, s32[]{:T(128)}, f32[1536]{0:T(1024)S(1)}, /*index=5*/f32[1,512]{1,0:T(1,128)S(1)},...) while((s32[]{:T(128)}, f32[512,512]{1,0:T(8,128)S(1)}, ...), condition=%wide.region_11.10_spmd, body=%wide.region_10.9_spmd.sunk | while | flops 270795776 | bytes 25233092 | solution.py:65
  156.4 4.6 %reshape.89 = f32[512,1025]{1,0:T(8,128)} reshape(f32[524800]{0:T(1024)} %bitcast.56) | data formatting | bytes 4198400 | tf_op jit(solution)/shard_map/while/body/eval_jaxpr/while/body/eval_jaxpr/while/body/reshape | solution.py:19
  177.4 28.6 %while.177 = (s32[]{:T(128)}, f32[512,512]{1,0:T(8,128)S(1)}, s32[]{:T(128)}, s32[]{:T(128)}, f32[1536]{0:T(1024)S(1)}, /*index=5*/f32[1,512]{1,0:T(1,128)S(1)},...) while((s32[]{:T(128)}, f32[512,512]{1,0:T(8,128)S(1)}, ...), condition=%wide.region_11.10_spmd, body=%wide.region_10.9_spmd.sunk | while | flops 270795776 | bytes 25233092 | solution.py:65
  179.4 4.6 %reshape.89 = f32[512,1025]{1,0:T(8,128)} reshape(f32[524800]{0:T(1024)} %bitcast.56) | data formatting | bytes 4198400 | tf_op jit(solution)/shard_map/while/body/eval_jaxpr/while/body/eval_jaxpr/while/body/reshape | solution.py:19
  215.5 60.5 %while.176 = (s32[]{:T(128)}, f32[2,8192]{1,0:T(2,128)}, f32[2,8192]{1,0:T(2,128)}, s32[]{:T(128)}, s32[]{:T(128)}, /*index=5*/s32[]{:T(128)}, s32[2]{0:T(128)},...) while((s32[]{:T(128)}, f32[2,8192]{1,0:T(2,128)}, ...), condition=%wide.region_14.14_spmd, body=%wide.region_9.13_spmd.sunk | while | flops 272631840 | bytes 27380040 | solution.py:143
  218.4 14.3 %while.177 = (s32[]{:T(128)}, f32[512,512]{1,0:T(8,128)S(1)}, s32[]{:T(128)}, s32[]{:T(128)}, f32[1536]{0:T(1024)S(1)}, /*index=5*/f32[1,512]{1,0:T(1,128)S(1)},...) while((s32[]{:T(128)}, f32[512,512]{1,0:T(8,128)S(1)}, ...), condition=%wide.region_11.10_spmd, body=%wide.region_10.9_spmd.sunk | while | flops 270795776 | bytes 25233092 | solution.py:65
  241.5 28.6 %while.177 = (s32[]{:T(128)}, f32[512,512]{1,0:T(8,128)S(1)}, s32[]{:T(128)}, s32[]{:T(128)}, f32[1536]{0:T(1024)S(1)}, /*index=5*/f32[1,512]{1,0:T(1,128)S(1)},...) while((s32[]{:T(128)}, f32[512,512]{1,0:T(8,128)S(1)}, ...), condition=%wide.region_11.10_spmd, body=%wide.region_10.9_spmd.sunk | while | flops 270795776 | bytes 25233092 | solution.py:65
  279.5 60.4 %while.176 = (s32[]{:T(128)}, f32[2,8192]{1,0:T(2,128)}, f32[2,8192]{1,0:T(2,128)}, s32[]{:T(128)}, s32[]{:T(128)}, /*index=5*/s32[]{:T(128)}, s32[2]{0:T(128)},...) while((s32[]{:T(128)}, f32[2,8192]{1,0:T(2,128)}, ...), condition=%wide.region_14.14_spmd, body=%wide.region_9.13_spmd.sunk | while | flops 272631840 | bytes 27380040 | solution.py:143
  282.5 14.3 %while.177 = (s32[]{:T(128)}, f32[512,512]{1,0:T(8,128)S(1)}, s32[]{:T(128)}, s32[]{:T(128)}, f32[1536]{0:T(1024)S(1)}, /*index=5*/f32[1,512]{1,0:T(1,128)S(1)},...) while((s32[]{:T(128)}, f32[512,512]{1,0:T(8,128)S(1)}, ...), condition=%wide.region_11.10_spmd, body=%wide.region_10.9_spmd.sunk | while | flops 270795776 | bytes 25233092 | solution.py:65
  305.5 28.6 %while.177 = (s32[]{:T(128)}, f32[512,512]{1,0:T(8,128)S(1)}, s32[]{:T(128)}, s32[]{:T(128)}, f32[1536]{0:T(1024)S(1)}, /*index=5*/f32[1,512]{1,0:T(1,128)S(1)},...) while((s32[]{:T(128)}, f32[512,512]{1,0:T(8,128)S(1)}, ...), condition=%wide.region_11.10_spmd, body=%wide.region_10.9_spmd.sunk | while | flops 270795776 | bytes 25233092 | solution.py:65
  343.6 60.5 %while.176 = (s32[]{:T(128)}, f32[2,8192]{1,0:T(2,128)}, f32[2,8192]{1,0:T(2,128)}, s32[]{:T(128)}, s32[]{:T(128)}, /*index=5*/s32[]{:T(128)}, s32[2]{0:T(128)},...) while((s32[]{:T(128)}, f32[2,8192]{1,0:T(2,128)}, ...), condition=%wide.region_14.14_spmd, body=%wide.region_9.13_spmd.sunk | while | flops 272631840 | bytes 27380040 | solution.py:143
  346.5 14.3 %while.177 = (s32[]{:T(128)}, f32[512,512]{1,0:T(8,128)S(1)}, s32[]{:T(128)}, s32[]{:T(128)}, f32[1536]{0:T(1024)S(1)}, /*index=5*/f32[1,512]{1,0:T(1,128)S(1)},...) while((s32[]{:T(128)}, f32[512,512]{1,0:T(8,128)S(1)}, ...), condition=%wide.region_11.10_spmd, body=%wide.region_10.9_spmd.sunk | while | flops 270795776 | bytes 25233092 | solution.py:65
  369.6 28.6 %while.177 = (s32[]{:T(128)}, f32[512,512]{1,0:T(8,128)S(1)}, s32[]{:T(128)}, s32[]{:T(128)}, f32[1536]{0:T(1024)S(1)}, /*index=5*/f32[1,512]{1,0:T(1,128)S(1)},...) while((s32[]{:T(128)}, f32[512,512]{1,0:T(8,128)S(1)}, ...), condition=%wide.region_11.10_spmd, body=%wide.region_10.9_spmd.sunk | while | flops 270795776 | bytes 25233092 | solution.py:65
  404.1 10.3 %all_to_all.10 = f32[2,16,512]{2,0,1:T(2,128)S(1)} all-to-all(f32[2,16,512]{2,0,1:T(2,128)} %bitcast.67), channel_id=1, replica_groups=mesh['len'=2,'tile'=16] {'tile'}, dimensions={1} | all-to-all | bytes 131072 | tf_op jit(solution)/shard_map/all_to_all | solution.py:153
  (304 shorter events, 288.4 us)
Async XLA Ops:
  66.4 0.6 copy-start
  154.3 15.0 %copy-start.1 = (s32[2]{0:T(128)S(1)}, s32[2]{0:T(128)}, u32[]{:S(2)}) copy-start(s32[2]{0:T(128)} %get-tuple-element.1638) | copy-start | bytes 28 | tf_op jit(solution)/shard_map/while/body/eval_jaxpr/while
  177.4 29.3 %copy-start.1 = (s32[2]{0:T(128)S(1)}, s32[2]{0:T(128)}, u32[]{:S(2)}) copy-start(s32[2]{0:T(128)} %get-tuple-element.1638) | copy-start | bytes 28 | tf_op jit(solution)/shard_map/while/body/eval_jaxpr/while
  218.4 15.0 %copy-start.1 = (s32[2]{0:T(128)S(1)}, s32[2]{0:T(128)}, u32[]{:S(2)}) copy-start(s32[2]{0:T(128)} %get-tuple-element.1638) | copy-start | bytes 28 | tf_op jit(solution)/shard_map/while/body/eval_jaxpr/while
  241.5 29.3 %copy-start.1 = (s32[2]{0:T(128)S(1)}, s32[2]{0:T(128)}, u32[]{:S(2)}) copy-start(s32[2]{0:T(128)} %get-tuple-element.1638) | copy-start | bytes 28 | tf_op jit(solution)/shard_map/while/body/eval_jaxpr/while
  282.4 15.0 %copy-start.1 = (s32[2]{0:T(128)S(1)}, s32[2]{0:T(128)}, u32[]{:S(2)}) copy-start(s32[2]{0:T(128)} %get-tuple-element.1638) | copy-start | bytes 28 | tf_op jit(solution)/shard_map/while/body/eval_jaxpr/while
  305.5 29.3 %copy-start.1 = (s32[2]{0:T(128)S(1)}, s32[2]{0:T(128)}, u32[]{:S(2)}) copy-start(s32[2]{0:T(128)} %get-tuple-element.1638) | copy-start | bytes 28 | tf_op jit(solution)/shard_map/while/body/eval_jaxpr/while
  346.5 15.0 %copy-start.1 = (s32[2]{0:T(128)S(1)}, s32[2]{0:T(128)}, u32[]{:S(2)}) copy-start(s32[2]{0:T(128)} %get-tuple-element.1638) | copy-start | bytes 28 | tf_op jit(solution)/shard_map/while/body/eval_jaxpr/while
  369.6 29.3 %copy-start.1 = (s32[2]{0:T(128)S(1)}, s32[2]{0:T(128)}, u32[]{:S(2)}) copy-start(s32[2]{0:T(128)} %get-tuple-element.1638) | copy-start | bytes 28 | tf_op jit(solution)/shard_map/while/body/eval_jaxpr/while
  414.4 10.4 %all-to-all-start.1 = ((f32[2,16,512]{2,0,1:T(2,128)}), f32[2,16,512]{2,0,1:T(2,128)S(1)}, u32[]{:S(2)}, u32[]{:S(2)}) async-start(f32[2,16,512]{2,0,1:T(2,128)} %bitcast.68), calls=%async_computation.1 | async-start | bytes 131072 | tf_op jit(solution)/shard_map/all_to_all | solution.py:160
where the time goes:
time: 434 us; the launch traced here: 430 us
  local copies, waits for them, and re-layouts  234 us (54%)
  blocking collectives  120 us (28%)
  other arithmetic  27.3 us (6%)
  matrix products  22.6 us (5%)
  loops' own time  19.7 us (5%)
    reshape x30, local copies, waits for them, and re-layouts, shifted_block(): return repeated.reshape(columns, stride)[:, :positions]  112 us
    unnamed x1, blocking collectives  63 us
    another operation x60, local copies, waits for them, and re-layouts, shifted_block(): repeated = jnp.tile(window, columns + 1)[:columns * stride]  57.1 us
    dot_general x12, matrix products, add_block(): lax.dot_general(row_normal, col_normal, (((0,), (0,)), ((), ())), preferr...  22.6 us
    all_gather x1, blocking collectives, shared_stats(): lax.all_gather(inverses, 'tile', axis=1, tiled=True)  20.6 us
    all_gather x1, blocking collectives, shared_stats(): lax.all_gather(centres, 'tile', axis=1, tiled=True)  17.3 us
    dynamic_update_slice x8, local copies, waits for them, and re-layouts, per_length(): lax.dynamic_update_slice(left_best, jnp.minimum(left_old, left_min[None,...  10.7 us
    dynamic_update_slice x8, local copies, waits for them, and re-layouts, per_length(): lax.dynamic_update_slice(right_lowest_distance, jnp.minimum(right_old, ri...  10.6 us
  transfers between devices with their start and end apart: 1, of which 1 were waited for; matrix products, arithmetic and copies ran while one was open for 0% of the time, Pallas kernels for 0%

commit v1 on v0

v1 whole, which is shorter than its diff:
```python
import functools

import jax
import jax.numpy as jnp
from jax import lax
from jax.experimental import pallas as pl
from jax.experimental.pallas import tpu as pltpu
from jax.sharding import PartitionSpec as P

MAX_LEN = 1024
TILE_SIDE = 512
LANES = 128
CHUNK = 256

EMPTY_VALUE = 2.0
VAR_EPS = 1e-05

VMEM = pltpu.MemorySpace.VMEM
SMEM = pltpu.MemorySpace.SMEM


def gather_kernel(n, piece_ref, slots_ref, send_sem, recv_sem, own_sem):
    me = lax.axis_index("tile")
    barrier = pltpu.get_barrier_semaphore()

    def greet(step, carry):
        peer = lax.rem(me + step, n)
        pl.semaphore_signal(
            barrier, inc=1, device_id={"tile": peer}, device_id_type=pl.DeviceIdType.MESH
        )
        return carry

    lax.fori_loop(1, n, greet, 0)
    own = pltpu.make_async_copy(piece_ref, slots_ref.at[me], own_sem)
    own.start()
    pl.semaphore_wait(barrier, n - 1)

    def copy(step):
        peer = lax.rem(me + step, n)
        return pltpu.make_async_remote_copy(
            src_ref=piece_ref,
            dst_ref=slots_ref.at[me],
            send_sem=send_sem.at[step],
            recv_sem=recv_sem.at[step],
            device_id={"tile": peer},
            device_id_type=pl.DeviceIdType.MESH,
        )

    def send(step, carry):
        copy(step).start()
        return carry

    def finish(step, carry):
        copy(step).wait()
        return carry

    lax.fori_loop(1, n, send, 0)
    own.wait()
    lax.fori_loop(1, n, finish, 0)


def exchange_kernel(count_len, n, best_ref, parts_ref, send_sem, recv_sem, own_sem):
    total = count_len * n
    my_len = lax.axis_index("len")
    my_tile = lax.axis_index("tile")
    me = my_len * n + my_tile
    barrier = pltpu.get_barrier_semaphore()

    def where(step):
        peer = lax.rem(me + step, total)
        return peer // n, lax.rem(peer, n)

    def greet(step, carry):
        peer_len, peer_tile = where(step)
        pl.semaphore_signal(
            barrier,
            inc=1,
            device_id={"len": peer_len, "tile": peer_tile},
            device_id_type=pl.DeviceIdType.MESH,
        )
        return carry

    lax.fori_loop(1, total, greet, 0)
    own = pltpu.make_async_copy(best_ref.at[my_tile], parts_ref.at[me], own_sem)
    own.start()
    pl.semaphore_wait(barrier, total - 1)

    def copy(step):
        peer_len, peer_tile = where(step)
        return pltpu.make_async_remote_copy(
            src_ref=best_ref.at[peer_tile],
            dst_ref=parts_ref.at[me],
            send_sem=send_sem.at[step],
            recv_sem=recv_sem.at[step],
            device_id={"len": peer_len, "tile": peer_tile},
            device_id_type=pl.DeviceIdType.MESH,
        )

    def send(step, carry):
        copy(step).start()
        return carry

    def finish(step, carry):
        copy(step).wait()
        return carry

    lax.fori_loop(1, total, send, 0)
    own.wait()
    lax.fori_loop(1, total, finish, 0)


def sweep_kernel(
    piece,
    count_len,
    tile_ref,
    length_ref,
    barrier_ref,
    slots_ref,
    best_ref,
    line,
    base,
    full_mean,
    full_spread,
    part_mean,
    part_spread,
    centre_ref,
    inverse_ref,
    left_op,
    right_op,
):
    n = slots_ref.shape[0]
    width = line.shape[1]
    columns = width // LANES
    padded = slots_ref.shape[2]
    blocks = best_ref.shape[0]
    groups = blocks * (TILE_SIDE // LANES)
    reach = MAX_LEN // LANES

    line[...] = jnp.zeros(line.shape, jnp.float32)
    for t in range(n):
        start = t * piece
        low, shift = start // LANES * LANES, start % LANES
        room = min(padded + LANES, width - low)
        row = jnp.concatenate([slots_ref[t], jnp.zeros((1, LANES), jnp.float32)], axis=1)
        if shift:
            row = pltpu.roll(row, shift, 1)
        line[:, low : low + room] += row[:, :room]

    rows8 = jnp.broadcast_to(line[...], (8, width))
    sub = lax.broadcasted_iota(jnp.int32, (8, width), 0)
    for bit in (1, 2, 4):
        rows8 = jnp.where((sub & bit) != 0, pltpu.roll(rows8, width - bit, 1), rows8)
    for g in range(LANES // 8):
        base[8 * g : 8 * g + 8, :] = rows8 if g == 0 else pltpu.roll(rows8, width - 8 * g, 1)

    row_ids = lax.broadcasted_iota(jnp.int32, (LANES, LANES), 0)
    rests = [lax.rem(length_ref[l], LANES) for l in range(count_len)]
    scales = [1.0 / jnp.maximum(rest, 1).astype(jnp.float32) for rest in rests]

    def column_stats(a, carry):
        values = base[:, pl.ds(pl.multiple_of(a * LANES, LANES), LANES)]
        mean = jnp.sum(values, axis=0, keepdims=True) * (1.0 / LANES)
        off = values - mean
        full_mean[pl.ds(a, 1), :] = mean
        full_spread[pl.ds(a, 1), :] = jnp.sum(off * off, axis=0, keepdims=True)
        for l in range(count_len):
            inside = row_ids < rests[l]
            mean = jnp.sum(jnp.where(inside, values, 0.0), axis=0, keepdims=True) * scales[l]
            off = jnp.where(inside, values - mean, 0.0)
            part_mean[l, pl.ds(a, 1), :] = mean
            part_spread[l, pl.ds(a, 1), :] = jnp.sum(off * off, axis=0, keepdims=True)
        return carry

    lax.fori_loop(0, columns, column_stats, 0)

    for l in range(count_len):
        length = length_ref[l]
        size = length.astype(jnp.float32)
        whole = length // LANES
        rest = rests[l].astype(jnp.float32)
        rest_mean = part_mean[l, pl.ds(whole, groups), :]
        total = rest_mean * rest
        for k in range(reach):
            total += jnp.where(k < whole, full_mean[k : k + groups, :] * float(LANES), 0.0)
        centre = total / size
        gap = rest_mean - centre
        spread = part_spread[l, pl.ds(whole, groups), :] + rest * (gap * gap)
        for k in range(reach):
            gap = full_mean[k : k + groups, :] - centre
            spread += jnp.where(
                k < whole, full_spread[k : k + groups, :] + float(LANES) * (gap * gap), 0.0
            )
        centre_ref[l] = centre
        inverse_ref[l] = 1.0 / jnp.sqrt(spread / size + VAR_EPS)

    best_ref[...] = jnp.full(best_ref.shape, EMPTY_VALUE, jnp.float32)
    quarters = TILE_SIDE // LANES
    ratio = CHUNK // LANES

    def one_product(index, carry):
        slot, l = index // count_len, lax.rem(index, count_len)
        row_block, col_block = tile_ref[slot, 0], tile_ref[slot, 1]
        length, barrier = length_ref[l], barrier_ref[l]
        size = length.astype(jnp.float32)
        chunks = (length + CHUNK - 1) // CHUNK
        row_first, col_first = row_block * quarters, col_block * quarters

        stats = jnp.concatenate(
            [centre_ref[l, pl.ds(row_first, quarters), :], inverse_ref[l, pl.ds(row_first, quarters), :]],
            axis=0,
        )
        turned = jnp.transpose(stats)
        row_centre = [jnp.broadcast_to(turned[:, q : q + 1], (LANES, LANES)) for q in range(quarters)]
        row_inverse = [
            jnp.broadcast_to(turned[:, quarters + q : quarters + q + 1], (LANES, LANES))
            for q in range(quarters)
        ]
        lane_ids = lax.broadcasted_iota(jnp.int32, (LANES, LANES), 1)
        col_centre = [centre_ref[l, pl.ds(col_first + u, 1), :] for u in range(quarters)]
        col_inverse = [inverse_ref[l, pl.ds(col_first + u, 1), :] for u in range(quarters)]

        def fill(k, carry):
            here = pl.ds(pl.multiple_of(k * LANES, LANES), LANES)
            inside = lane_ids + k * LANES < length
            for q in range(quarters):
                spot = pl.multiple_of((row_first + q + k) * LANES, LANES)
                values = (base[:, pl.ds(spot, LANES)] - row_centre[q]) * row_inverse[q]
                left_op[q * LANES : (q + 1) * LANES, here] = jnp.where(inside, values, 0.0).astype(
                    jnp.bfloat16
                )
                spot = pl.multiple_of((col_first + q + k) * LANES, LANES)
                values = (base[:, pl.ds(spot, LANES)] - col_centre[q]) * col_inverse[q]
                right_op[here, q * LANES : (q + 1) * LANES] = values.astype(jnp.bfloat16)
            return carry

        lax.fori_loop(0, chunks * ratio, fill, 0)

        def finish(depth):
            product = jnp.dot(
                left_op[:, :depth], right_op[:depth, :], preferred_element_type=jnp.float32
            )
            ahead = (
                lax.broadcasted_iota(jnp.int32, product.shape, 1)
                - lax.broadcasted_iota(jnp.int32, product.shape, 0)
            )
            limit = barrier - (col_block - row_block) * TILE_SIDE
            product = jnp.where(ahead > limit, product, -size)
            col_best = jnp.max(product, axis=0, keepdims=True)
            folded = product[:, :LANES]
            for u in range(1, quarters):
                folded = jnp.maximum(folded, product[:, u * LANES : (u + 1) * LANES])
            row_best = jnp.concatenate(
                [
                    jnp.max(
                        jnp.transpose(folded[q * LANES : (q + 1) * LANES, :]), axis=0, keepdims=True
                    )
                    for q in range(quarters)
                ],
                axis=1,
            )
            spot = (row_block, pl.ds(l, 1))
            best_ref[spot] = jnp.minimum(best_ref[spot], 1.0 - row_best / size)
            spot = (col_block, pl.ds(count_len + l, 1))
            best_ref[spot] = jnp.minimum(best_ref[spot], 1.0 - col_best / size)

        for count in range(1, MAX_LEN // CHUNK + 1):

            @pl.when(chunks == count)
            def _():
                finish(count * CHUNK)

        return carry

    lax.fori_loop(0, tile_ref.shape[0] * count_len, one_product, 0)


def shards(series, window_lengths, exclusion, tile_list):
    n = lax.axis_size("tile")
    len_devices = lax.axis_size("len")
    count_len = window_lengths.shape[0]
    piece = series.shape[0]
    points = piece * n
    positions = points - MAX_LEN
    blocks = positions // TILE_SIDE
    padded = (piece + LANES - 1) // LANES * LANES
    columns = points // LANES
    groups = positions // LANES
    row = jnp.pad(series, (0, padded - piece)).reshape(1, padded)

    slots = pl.pallas_call(
        functools.partial(gather_kernel, n),
        out_shape=jax.ShapeDtypeStruct((n, 1, padded), jnp.float32),
        in_specs=[pl.BlockSpec(memory_space=VMEM)],
        out_specs=pl.BlockSpec(memory_space=VMEM),
        scratch_shapes=[
            pltpu.SemaphoreType.DMA((n,)),
            pltpu.SemaphoreType.DMA((n,)),
            pltpu.SemaphoreType.DMA,
        ],
        compiler_params=pltpu.CompilerParams(collective_id=0, has_side_effects=True),
        name="gather_series",
    )(row)

    best = pl.pallas_call(
        functools.partial(sweep_kernel, piece, count_len),
        out_shape=jax.ShapeDtypeStruct((blocks, 2 * count_len, TILE_SIDE), jnp.float32),
        in_specs=[
            pl.BlockSpec(memory_space=SMEM),
            pl.BlockSpec(memory_space=SMEM),
            pl.BlockSpec(memory_space=SMEM),
            pl.BlockSpec(memory_space=VMEM),
        ],
        out_specs=pl.BlockSpec(memory_space=VMEM),
        scratch_shapes=[
            pltpu.VMEM((1, points), jnp.float32),
            pltpu.VMEM((LANES, points), jnp.float32),
            pltpu.VMEM((columns, LANES), jnp.float32),
            pltpu.VMEM((columns, LANES), jnp.float32),
            pltpu.VMEM((count_len, columns + 8, LANES), jnp.float32),
            pltpu.VMEM((count_len, columns + 8, LANES), jnp.float32),
            pltpu.VMEM((count_len, groups, LANES), jnp.float32),
            pltpu.VMEM((count_len, groups, LANES), jnp.float32),
            pltpu.VMEM((TILE_SIDE, MAX_LEN), jnp.bfloat16),
            pltpu.VMEM((MAX_LEN, TILE_SIDE), jnp.bfloat16),
        ],
        name="sweep_tiles",
    )(tile_list, window_lengths, exclusion, slots)

    total = len_devices * n
    parts = pl.pallas_call(
        functools.partial(exchange_kernel, len_devices, n),
        out_shape=jax.ShapeDtypeStruct((total, 2 * count_len, TILE_SIDE), jnp.float32),
        in_specs=[pl.BlockSpec(memory_space=VMEM)],
        out_specs=pl.BlockSpec(memory_space=VMEM),
        scratch_shapes=[
            pltpu.SemaphoreType.DMA((total,)),
            pltpu.SemaphoreType.DMA((total,)),
            pltpu.SemaphoreType.DMA,
        ],
        compiler_params=pltpu.CompilerParams(collective_id=1, has_side_effects=True),
        name="exchange_minima",
    )(best)
    merged = jnp.min(parts.reshape(len_devices, n, 2, count_len, TILE_SIDE), axis=1)
    right = merged[:, 0].reshape(len_devices * count_len, TILE_SIDE)
    left = merged[:, 1].reshape(len_devices * count_len, TILE_SIDE)
    return (right, left)


def solution(mesh):
    return jax.shard_map(
        shards,
        mesh=mesh,
        in_specs=(P("tile"), P("len"), P("len"), P("tile", None)),
        out_specs=(P(None, "tile"), P(None, "tile")),
        check_vma=False,
    )
```

time: 434 us -> 49.8 us (0.11)
  local copies, waits for them, and re-layouts: 234 us -> 4.99 us
  blocking collectives: 120 us -> 0 us
  Pallas kernels: 0 us -> 44 us
  other arithmetic: 27.3 us -> 0.09 us
  matrix products: 22.6 us -> 0 us
  loops' own time: 19.7 us -> 0 us
    reshape x30 -> x2, local copies, waits for them, and re-layouts: 112 us -> 1.74 us  [the longest x1 1.15 us: shards(): parts.reshape(len_devices, n, 2, count_len, TILE_SIDE)]
    unnamed x1 -> x0, blocking collectives: 63 us -> none
    another operation x72 -> x2, local copies, waits for them, and re-layouts: 58.1 us -> 1.23 us  [the longest x1 0.61 us: shards(): left = merged[:, 1].reshape(len_devices * count_len, TILE_SIDE)]
    all_gather x4 -> x0, blocking collectives: 46.6 us -> none  [the longest x1 20.6 us: shared_stats(): lax.all_gather(inverses, 'tile', axis=1, tiled=True)]
    pallas_call x0 -> x3, Pallas kernels: none -> 44 us  [the longest x1 21.3 us: shards(): pl.pallas_call(functools.partial(sweep_kernel, piece, count_len), out_sha...]
    dynamic_slice x73 -> x0, local copies, waits for them, and re-layouts: 36.3 us -> none  [the longest x8 10.3 us: per_length(): length = lengths[length_index]]
    dot_general x12 -> x0, matrix products: 22.6 us -> none  [add_block(): lax.dot_general(row_normal, col_normal, (((0,), (0,)), ((), ())), preferr...]
    dynamic_update_slice x20 -> x0, local copies, waits for them, and re-layouts: 21.5 us -> none  [the longest x8 10.7 us: per_length(): lax.dynamic_update_slice(left_best, jnp.minimum(left_old, left_min[None,...]
  transfers between devices with their start and end apart: 1 -> 0, of which waited for: 1 -> 0; matrix products, arithmetic and copies ran while one was open for 0% -> 0% of each run, Pallas kernels for 0% -> 0%
where the time goes in v1:
time: 49.8 us; the launch traced here: 49.7 us
  Pallas kernels  44 us (88%)
  local copies, waits for them, and re-layouts  4.99 us (10%)
  between operations  0.66 us (1%)
    pallas_call x1, Pallas kernels, shards(): pl.pallas_call(functools.partial(sweep_kernel, piece, count_len), out_sha...  21.3 us
    pallas_call x1, Pallas kernels, shards(): pl.pallas_call(functools.partial(exchange_kernel, len_devices, n), out_sh...  12.7 us
    pallas_call x1, Pallas kernels, shards(): pl.pallas_call(functools.partial(gather_kernel, n), out_shape=jax.ShapeDt...  10 us
    unnamed x1, local copies, waits for them, and re-layouts  1.34 us
    reshape x1, local copies, waits for them, and re-layouts, shards(): parts.reshape(len_devices, n, 2, count_len, TILE_SIDE)  1.15 us

profile of v1, /device:TPU:0, one launch (start us, length us, event | category | flops | bytes accessed | tf_op | source)
XLA Modules:
  0.0 49.7 jit_solution(18340247058199986447)
XLA Ops:
  0.6 1.3 %copy.7.tile_ref = s32[4,2]{1,0:T(4,128)} copy(s32[4,2]{0,1:T(2,128)} %param.7) | data formatting | bytes 64 | tf_op args[3]
  2.0 0.7 %pad.4 = f32[640]{0:T(1024)S(1)} pad(f32[576]{0:T(1024)} %param.4, f32[]{:T(128)} %constant.1.clone.1), padding=0_64 | pad | bytes 4868 | tf_op jit(solution)/shard_map/jit(_pad)/pad | solution.py:288
  2.7 0.6 %reshape.10.piece_ref = f32[1,640]{1,0:T(1,128)} reshape(f32[640]{0:T(1024)S(1)} %pad.4) | data formatting | bytes 5120 | tf_op jit(solution)/shard_map/reshape | solution.py:288
  3.2 10.0 %gather_series.1.slots_ref = f32[16,1,640]{2,1,0:T(1,128)} custom-call(f32[1,640]{1,0:T(1,128)} %reshape.10.piece_ref), custom_call_target="tpu_custom_call" | custom-call | tf_op jit(solution)/shard_map/gather_series/pallas_call | solution.py:290
  13.2 21.3 %sweep_tiles.1.best_ref = f32[16,4,512]{2,1,0:T(4,128)} custom-call(s32[4,2]{1,0:T(4,128)} %copy.7.tile_ref, s32[2]{0:T(128)} %length_ref.1, s32[2]{0:T(128)} %barrier_ref.1, f32[16,1,640]{2,1,0:T(1,128)} %gather_series.1.slots_ref), custom_call_target="tpu_custom_call" | custom-call | tf_op jit(solution)/shard_map/sweep_tiles/pallas_call | solution.py:304
  34.6 12.7 %exchange_minima.1 = f32[32,4,512]{2,1,0:T(4,128)} custom-call(f32[16,4,512]{2,1,0:T(4,128)} %sweep_tiles.1.best_ref), custom_call_target="tpu_custom_call" | custom-call | tf_op jit(solution)/shard_map/exchange_minima/pallas_call | solution.py:330
  47.3 1.2 %reshape.11 = f32[2,16,2,2,512]{4,3,2,1,0:T(2,128)S(1)} reshape(f32[32,4,512]{2,1,0:T(4,128)} %exchange_minima.1) | data formatting | bytes 524288 | tf_op jit(solution)/shard_map/reshape | solution.py:343
  48.4 0.1 reduce_min.9
  48.5 0.6 %reshape_squeeze.7 = f32[4,512]{1,0:T(4,128)} reshape(f32[2,1,2,512]{3,2,1,0:T(2,128)S(1)} %get-tuple-element.2) | data formatting | bytes 16384 | tf_op jit(solution)/shard_map/reshape;squeeze | solution.py:345
  49.1 0.6 %reshape_squeeze.6 = f32[4,512]{1,0:T(4,128)} reshape(f32[2,1,2,512]{3,2,1,0:T(2,128)S(1)} %get-tuple-element.3) | data formatting | bytes 16384 | tf_op jit(solution)/shard_map/reshape;squeeze | solution.py:344
  (1 shorter events, 0.0 us)

commit v2 on v1

v2 whole, which is shorter than its diff:
```python
import functools

import jax
import jax.numpy as jnp
from jax import lax
from jax.experimental import pallas as pl
from jax.experimental.pallas import tpu as pltpu
from jax.sharding import PartitionSpec as P

MAX_LEN = 1024
TILE_SIDE = 512
LANES = 128
CHUNK = 256

EMPTY_VALUE = 2.0
VAR_EPS = 1e-05

VMEM = pltpu.MemorySpace.VMEM
SMEM = pltpu.MemorySpace.SMEM


def signal_all(barrier, axis, n):
    me = lax.axis_index(axis)
    for step in range(1, n):
        pl.semaphore_signal(
            barrier,
            inc=1,
            device_id={axis: lax.rem(me + step, n)},
            device_id_type=pl.DeviceIdType.MESH,
        )


def copy_to(axis, n, step, source, target, send_sem, recv_sem):
    peer = lax.rem(lax.axis_index(axis) + step, n)
    return pltpu.make_async_remote_copy(
        src_ref=source(peer),
        dst_ref=target,
        send_sem=send_sem.at[step],
        recv_sem=recv_sem.at[step],
        device_id={axis: peer},
        device_id_type=pl.DeviceIdType.MESH,
    )


def gather_kernel(n, piece_ref, slots_ref, send_sem, recv_sem, own_sem):
    me = lax.axis_index("tile")
    barrier = pltpu.get_barrier_semaphore()
    signal_all(barrier, "tile", n)
    own = pltpu.make_async_copy(piece_ref, slots_ref.at[me], own_sem)
    own.start()
    pl.semaphore_wait(barrier, n - 1)
    copies = [
        copy_to("tile", n, step, lambda peer: piece_ref, slots_ref.at[me], send_sem, recv_sem)
        for step in range(1, n)
    ]
    for copy in copies:
        copy.start()
    own.wait()
    for copy in copies:
        copy.wait()


def exchange_kernel(
    count_len,
    n,
    best_ref,
    right_ref,
    left_ref,
    parts,
    mine,
    groups,
    send_sem,
    recv_sem,
    own_sem,
    send_len,
    recv_len,
):
    my_len = lax.axis_index("len")
    my_tile = lax.axis_index("tile")
    rows = best_ref.shape[1] // 2
    barrier = pltpu.get_barrier_semaphore()
    signal_all(barrier, "tile", n)
    signal_all(barrier, "len", count_len)
    own = pltpu.make_async_copy(best_ref.at[my_tile], parts.at[my_tile], own_sem)
    own.start()
    pl.semaphore_wait(barrier, n - 1 + count_len - 1)
    copies = [
        copy_to(
            "tile", n, step, lambda peer: best_ref.at[peer], parts.at[my_tile], send_sem, recv_sem
        )
        for step in range(1, n)
    ]
    for copy in copies:
        copy.start()
    own.wait()
    for copy in copies:
        copy.wait_recv()
    merged = jnp.min(parts[...], axis=0)
    mine[...] = merged
    copies_len = [
        copy_to("len", count_len, step, lambda peer: mine, groups.at[my_len], send_len, recv_len)
        for step in range(1, count_len)
    ]
    for copy in copies_len:
        copy.start()
    groups[my_len] = merged
    for copy in copies:
        copy.wait_send()
    for copy in copies_len:
        copy.wait()
    for g in range(count_len):
        right_ref[g * rows : (g + 1) * rows, :] = groups[g, :rows, :]
        left_ref[g * rows : (g + 1) * rows, :] = groups[g, rows:, :]


def shifted(values, count):
    rows = values.shape[0]
    skip, shift = count // LANES, count % LANES
    if shift:
        lane_ids = lax.broadcasted_iota(jnp.int32, values.shape, 1)
        values = pltpu.roll(values, LANES - shift, 1)
        values = jnp.where(lane_ids < LANES - shift, values, pltpu.roll(values, rows - 1, 0))
    if skip:
        values = pltpu.roll(values, rows - skip, 0)
    return values


def window_stats(packed, lengths):
    mean, spread = packed, jnp.zeros_like(packed)
    results = [(jnp.zeros_like(packed), jnp.zeros_like(packed)) for _ in lengths]
    bits = MAX_LEN.bit_length()
    for b in range(bits):
        first = 1 << b
        for l, length in enumerate(lengths):
            tail_mean, tail_spread = results[l]
            if b:
                tail_mean, tail_spread = shifted(tail_mean, first), shifted(tail_spread, first)
            rest = lax.rem(length, first).astype(jnp.float32)
            share = rest / (rest + first)
            gap = tail_mean - mean
            taken = (length & first) != 0
            results[l] = (
                jnp.where(taken, mean + gap * share, results[l][0]),
                jnp.where(
                    taken, spread + tail_spread + gap * gap * (share * first), results[l][1]
                ),
            )
        if b < bits - 1:
            next_mean = shifted(mean, first)
            gap = next_mean - mean
            mean = 0.5 * (mean + next_mean)
            if b:
                spread = spread + shifted(spread, first) + gap * gap * (0.5 * first)
            else:
                spread = gap * gap * 0.5
    return [
        (mean, 1.0 / jnp.sqrt(spread / length.astype(jnp.float32) + VAR_EPS))
        for (mean, spread), length in zip(results, lengths)
    ]


def sweep_kernel(
    piece,
    count_len,
    tile_ref,
    length_ref,
    barrier_ref,
    slots_ref,
    best_ref,
    line,
    base,
    packed,
    centre_ref,
    inverse_ref,
    left_op,
    right_op,
):
    n = slots_ref.shape[0]
    width = line.shape[1]
    columns = width // LANES
    padded = slots_ref.shape[2]

    line[...] = jnp.zeros(line.shape, jnp.float32)
    for t in range(n):
        start = t * piece
        low, shift = start // LANES * LANES, start % LANES
        room = min(padded + LANES, width - low)
        row = jnp.concatenate([slots_ref[t], jnp.zeros((1, LANES), jnp.float32)], axis=1)
        if shift:
            row = pltpu.roll(row, shift, 1)
        line[:, low : low + room] += row[:, :room]
    for a in range(columns):
        packed[a : a + 1, :] = line[:, a * LANES : (a + 1) * LANES]

    lengths = [length_ref[l] for l in range(count_len)]
    for l, (centre, inverse) in enumerate(window_stats(packed[...], lengths)):
        centre_ref[l] = centre
        inverse_ref[l] = inverse

    rows8 = jnp.broadcast_to(line[...], (8, width))
    sub = lax.broadcasted_iota(jnp.int32, (8, width), 0)
    for bit in (1, 2, 4):
        rows8 = jnp.where((sub & bit) != 0, pltpu.roll(rows8, width - bit, 1), rows8)
    for g in range(LANES // 8):
        base[8 * g : 8 * g + 8, :] = rows8 if g == 0 else pltpu.roll(rows8, width - 8 * g, 1)

    best_ref[...] = jnp.full(best_ref.shape, EMPTY_VALUE, jnp.float32)
    quarters = TILE_SIDE // LANES

    def one_product(index, carry):
        slot, l = index // count_len, lax.rem(index, count_len)
        row_block, col_block = tile_ref[slot, 0], tile_ref[slot, 1]
        length, barrier = length_ref[l], barrier_ref[l]
        size = length.astype(jnp.float32)
        chunks = (length + CHUNK - 1) // CHUNK
        row_first, col_first = row_block * quarters, col_block * quarters
        limit = barrier - (col_block - row_block) * TILE_SIDE

        def finish(depth):
            turned = jnp.transpose(
                jnp.concatenate(
                    [
                        centre_ref[l, pl.ds(row_first, quarters), :],
                        inverse_ref[l, pl.ds(row_first, quarters), :],
                    ],
                    axis=0,
                )
            )
            col_centre, col_inverse = (
                jnp.concatenate(
                    [source[l, pl.ds(col_first + u, 1), :] for u in range(quarters)], axis=1
                )
                for source in (centre_ref, inverse_ref)
            )
            for k in range(depth // LANES):
                spot = pl.ds(pl.multiple_of((col_first + k) * LANES, LANES), TILE_SIDE)
                right_op[k * LANES : (k + 1) * LANES, :] = (
                    (base[:, spot] - col_centre) * col_inverse
                ).astype(jnp.bfloat16)
            sure = depth - CHUNK
            lane_ids = lax.broadcasted_iota(jnp.int32, (16, CHUNK), 1)
            inside = lane_ids < length - sure
            col_best = None
            row_best = []
            for half in range(0, quarters, 2):
                for q in range(half, half + 2):
                    spot = pl.ds(pl.multiple_of((row_first + q) * LANES, LANES), depth)
                    for g in range(0, LANES, 16):
                        values = (base[g : g + 16, spot] - turned[g : g + 16, q : q + 1]) * turned[
                            g : g + 16, quarters + q : quarters + q + 1
                        ]
                        last = jnp.where(inside, values[:, sure:], 0.0)
                        at = q * LANES + g
                        if sure:
                            left_op[at : at + 16, :sure] = values[:, :sure].astype(jnp.bfloat16)
                        left_op[at : at + 16, sure:depth] = last.astype(jnp.bfloat16)
                low = half * LANES
                product = jnp.dot(
                    left_op[low : low + 2 * LANES, :depth],
                    right_op[:depth, :],
                    preferred_element_type=jnp.float32,
                )
                ahead = lax.broadcasted_iota(jnp.int32, product.shape, 1) - (
                    lax.broadcasted_iota(jnp.int32, product.shape, 0) + low
                )
                product = jnp.where(ahead > limit, product, -size)
                top = jnp.max(product, axis=0, keepdims=True)
                col_best = top if col_best is None else jnp.maximum(col_best, top)
                folded = product[:, :LANES]
                for u in range(1, quarters):
                    folded = jnp.maximum(folded, product[:, u * LANES : (u + 1) * LANES])
                for q in range(2):
                    turned_back = jnp.transpose(folded[q * LANES : (q + 1) * LANES, :])
                    row_best.append(jnp.max(turned_back, axis=0, keepdims=True))
            row_best = jnp.concatenate(row_best, axis=1)
            spot = (row_block, pl.ds(l, 1))
            best_ref[spot] = jnp.minimum(best_ref[spot], 1.0 - row_best / size)
            spot = (col_block, pl.ds(count_len + l, 1))
            best_ref[spot] = jnp.minimum(best_ref[spot], 1.0 - col_best / size)

        for count in range(1, MAX_LEN // CHUNK + 1):

            @pl.when(chunks == count)
            def _():
                finish(count * CHUNK)

        return carry

    lax.fori_loop(0, tile_ref.shape[0] * count_len, one_product, 0)


def shards(series, window_lengths, exclusion, tile_list):
    n = lax.axis_size("tile")
    len_devices = lax.axis_size("len")
    count_len = window_lengths.shape[0]
    piece = series.shape[0]
    points = piece * n
    positions = points - MAX_LEN
    blocks = positions // TILE_SIDE
    padded = (piece + LANES - 1) // LANES * LANES
    columns = points // LANES
    row = jnp.pad(series, (0, padded - piece)).reshape(1, padded)

    slots = pl.pallas_call(
        functools.partial(gather_kernel, n),
        out_shape=jax.ShapeDtypeStruct((n, 1, padded), jnp.float32),
        in_specs=[pl.BlockSpec(memory_space=VMEM)],
        out_specs=pl.BlockSpec(memory_space=VMEM),
        scratch_shapes=[
            pltpu.SemaphoreType.DMA((n,)),
            pltpu.SemaphoreType.DMA((n,)),
            pltpu.SemaphoreType.DMA,
        ],
        compiler_params=pltpu.CompilerParams(collective_id=0, has_side_effects=True),
        name="gather_series",
    )(row)

    best = pl.pallas_call(
        functools.partial(sweep_kernel, piece, count_len),
        out_shape=jax.ShapeDtypeStruct((blocks, 2 * count_len, TILE_SIDE), jnp.float32),
        in_specs=[
            pl.BlockSpec(memory_space=SMEM),
            pl.BlockSpec(memory_space=SMEM),
            pl.BlockSpec(memory_space=SMEM),
            pl.BlockSpec(memory_space=VMEM),
        ],
        out_specs=pl.BlockSpec(memory_space=VMEM),
        scratch_shapes=[
            pltpu.VMEM((1, points), jnp.float32),
            pltpu.VMEM((LANES, points), jnp.float32),
            pltpu.VMEM((columns, LANES), jnp.float32),
            pltpu.VMEM((count_len, columns, LANES), jnp.float32),
            pltpu.VMEM((count_len, columns, LANES), jnp.float32),
            pltpu.VMEM((TILE_SIDE, MAX_LEN), jnp.bfloat16),
            pltpu.VMEM((MAX_LEN, TILE_SIDE), jnp.bfloat16),
        ],
        name="sweep_tiles",
    )(tile_list, window_lengths, exclusion, slots)

    block = (2 * count_len, TILE_SIDE)
    profile = jax.ShapeDtypeStruct((len_devices * count_len, TILE_SIDE), jnp.float32)
    return pl.pallas_call(
        functools.partial(exchange_kernel, len_devices, n),
        out_shape=(profile, profile),
        in_specs=[pl.BlockSpec(memory_space=VMEM)],
        out_specs=(pl.BlockSpec(memory_space=VMEM), pl.BlockSpec(memory_space=VMEM)),
        scratch_shapes=[
            pltpu.VMEM((n, *block), jnp.float32),
            pltpu.VMEM(block, jnp.float32),
            pltpu.VMEM((len_devices, *block), jnp.float32),
            pltpu.SemaphoreType.DMA((n,)),
            pltpu.SemaphoreType.DMA((n,)),
            pltpu.SemaphoreType.DMA,
            pltpu.SemaphoreType.DMA((len_devices,)),
            pltpu.SemaphoreType.DMA((len_devices,)),
        ],
        compiler_params=pltpu.CompilerParams(collective_id=1, has_side_effects=True),
        name="exchange_minima",
    )(best)


def solution(mesh):
    return jax.shard_map(
        shards,
        mesh=mesh,
        in_specs=(P("tile"), P("len"), P("len"), P("tile", None)),
        out_specs=(P(None, "tile"), P(None, "tile")),
        check_vma=False,
    )
```

time: 49.8 us -> 39 us (0.78); the launches traced: 49.7 us -> 38.4 us
  Pallas kernels: 44 us -> 33.3 us
    pallas_call x1, Pallas kernels: 21.3 us -> 11.2 us  [shards(): pl.pallas_call(functools.partial(sweep_kernel, piece, count_len), out_sha...]
    unnamed x1 -> x5, local copies, waits for them, and re-layouts: 1.34 us -> 3.24 us
    another operation x2 -> x0, local copies, waits for them, and re-layouts: 1.23 us -> none  [the longest x1 0.61 us: shards(): left = merged[:, 1].reshape(len_devices * count_len, TILE_SIDE)]
    reshape x1 -> x0, local copies, waits for them, and re-layouts: 1.15 us -> none  [shards(): parts.reshape(len_devices, n, 2, count_len, TILE_SIDE)]
    pallas_call x1, Pallas kernels: 12.7 us -> 12.1 us  [shards(): pl.pallas_call(functools.partial(exchange_kernel, len_devices, n), out_sh...]
where the time goes in v2:
time: 39 us; the launch traced here: 38.4 us
  Pallas kernels  33.3 us (85%)
  local copies, waits for them, and re-layouts  4.51 us (12%)
  between operations  0.66 us (2%)
    pallas_call x1, Pallas kernels, shards(): pl.pallas_call(functools.partial(exchange_kernel, len_devices, n), out_sh...  12.1 us
    pallas_call x1, Pallas kernels, shards(): pl.pallas_call(functools.partial(sweep_kernel, piece, count_len), out_sha...  11.2 us
    pallas_call x1, Pallas kernels, shards(): pl.pallas_call(functools.partial(gather_kernel, n), out_shape=jax.ShapeDt...  10 us
    unnamed x5, local copies, waits for them, and re-layouts  3.24 us

profile of v2, /device:TPU:0, one launch (start us, length us, event | category | flops | bytes accessed | tf_op | source)
XLA Modules:
  0.0 38.4 jit_solution(17937959936781018903)
XLA Ops:
  0.6 1.3 %copy.6.tile_ref = s32[4,2]{1,0:T(4,128)} copy(s32[4,2]{0,1:T(2,128)} %param.7) | data formatting | bytes 64 | tf_op args[3]
  2.0 0.7 %pad.4 = f32[640]{0:T(1024)S(1)} pad(f32[576]{0:T(1024)} %param.4, f32[]{:T(128)} %constant.2.clone.1), padding=0_64 | pad | bytes 4868 | tf_op jit(solution)/shard_map/jit(_pad)/pad | solution.py:302
  2.7 0.6 %reshape.7.piece_ref = f32[1,640]{1,0:T(1,128)} reshape(f32[640]{0:T(1024)S(1)} %pad.4) | data formatting | bytes 5120 | tf_op jit(solution)/shard_map/reshape | solution.py:302
  3.2 10.0 %gather_series.1.slots_ref = f32[16,1,640]{2,1,0:T(1,128)} custom-call(f32[1,640]{1,0:T(1,128)} %reshape.7.piece_ref), custom_call_target="tpu_custom_call" | custom-call | tf_op jit(solution)/shard_map/gather_series/pallas_call | solution.py:304
  13.2 11.2 %sweep_tiles.1.best_ref = f32[16,4,512]{2,1,0:T(4,128)} custom-call(s32[4,2]{1,0:T(4,128)} %copy.6.tile_ref, s32[2]{0:T(128)} %length_ref.1, s32[2]{0:T(128)} %barrier_ref.1, f32[16,1,640]{2,1,0:T(1,128)} %gather_series.1.slots_ref), custom_call_target="tpu_custom_call" | custom-call | tf_op jit(solution)/shard_map/sweep_tiles/pallas_call | solution.py:318
  24.4 12.1 %exchange_minima.1 = (f32[4,512]{1,0:T(4,128)}, f32[4,512]{1,0:T(4,128)}) custom-call(f32[16,4,512]{2,1,0:T(4,128)} %sweep_tiles.1.best_ref), custom_call_target="tpu_custom_call" | custom-call | tf_op jit(solution)/shard_map/exchange_minima/pallas_call | solution.py:342
  36.5 0.0 copy-start
  36.5 1.3 %copy.9 = f32[4,512]{1,0:T(4,128)} copy(f32[4,512]{1,0:T(4,128)} %get-tuple-element.4) | data formatting | bytes 16384
  37.8 0.0 copy-done
  37.8 0.6 %copy.10 = f32[4,512]{1,0:T(4,128)} copy(f32[4,512]{1,0:T(4,128)S(1)} %copy-done) | data formatting | bytes 16384
Async XLA Ops:
  36.5 1.3 %copy-start = (f32[4,512]{1,0:T(4,128)S(1)}, f32[4,512]{1,0:T(4,128)}, u32[]{:S(2)}) copy-start(f32[4,512]{1,0:T(4,128)} %get-tuple-element.5) | copy-start | bytes 24580

commit v3 on v2

--- a/solution.py
+++ b/solution.py
@@ -11,6 +11,8 @@
 TILE_SIDE = 512
 LANES = 128
 CHUNK = 256
+GRANT = 1 << 20
+FLAT = 1024
 
 EMPTY_VALUE = 2.0
 VAR_EPS = 1e-05
@@ -42,15 +44,19 @@
     )
 
 
-def gather_kernel(n, piece_ref, slots_ref, send_sem, recv_sem, own_sem):
+def gather_kernel(n, piece_ref, slots_ref, staged, send_sem, recv_sem, own_sem):
     me = lax.axis_index("tile")
+    stride = slots_ref.shape[0] // n
+    slot = slots_ref.at[pl.ds(pl.multiple_of(me * stride, FLAT), staged.shape[0])]
+    staged[...] = jnp.zeros(staged.shape, jnp.float32)
+    staged[: piece_ref.shape[0]] = piece_ref[...]
     barrier = pltpu.get_barrier_semaphore()
     signal_all(barrier, "tile", n)
-    own = pltpu.make_async_copy(piece_ref, slots_ref.at[me], own_sem)
+    own = pltpu.make_async_copy(staged, slot, own_sem)
     own.start()
     pl.semaphore_wait(barrier, n - 1)
     copies = [
-        copy_to("tile", n, step, lambda peer: piece_ref, slots_ref.at[me], send_sem, recv_sem)
+        copy_to("tile", n, step, lambda peer: staged, slot, send_sem, recv_sem)
         for step in range(1, n)
     ]
     for copy in copies:
@@ -175,17 +181,19 @@
     left_op,
     right_op,
 ):
-    n = slots_ref.shape[0]
     width = line.shape[1]
     columns = width // LANES
-    padded = slots_ref.shape[2]
+    n = width // piece
+    stride = slots_ref.shape[0] // n
+    padded = (piece + LANES - 1) // LANES * LANES
 
     line[...] = jnp.zeros(line.shape, jnp.float32)
     for t in range(n):
         start = t * piece
         low, shift = start // LANES * LANES, start % LANES
         room = min(padded + LANES, width - low)
-        row = jnp.concatenate([slots_ref[t], jnp.zeros((1, LANES), jnp.float32)], axis=1)
+        row = slots_ref[t * stride : t * stride + padded].reshape(1, padded)
+        row = jnp.concatenate([row, jnp.zeros((1, LANES), jnp.float32)], axis=1)
         if shift:
             row = pltpu.roll(row, shift, 1)
         line[:, low : low + room] += row[:, :room]
@@ -209,7 +217,7 @@
 
     def one_product(index, carry):
         slot, l = index // count_len, lax.rem(index, count_len)
-        row_block, col_block = tile_ref[slot, 0], tile_ref[slot, 1]
+        row_block, col_block = tile_ref[0, slot], tile_ref[1, slot]
         length, barrier = length_ref[l], barrier_ref[l]
         size = length.astype(jnp.float32)
         chunks = (length + CHUNK - 1) // CHUNK
@@ -286,7 +294,7 @@
 
         return carry
 
-    lax.fori_loop(0, tile_ref.shape[0] * count_len, one_product, 0)
+    lax.fori_loop(0, tile_ref.shape[1] * count_len, one_product, 0)
 
 
 def shards(series, window_lengths, exclusion, tile_list):
@@ -297,23 +305,25 @@
     points = piece * n
     positions = points - MAX_LEN
     blocks = positions // TILE_SIDE
-    padded = (piece + LANES - 1) // LANES * LANES
+    stride = (piece + FLAT - 1) // FLAT * FLAT
     columns = points // LANES
-    row = jnp.pad(series, (0, padded - piece)).reshape(1, padded)
 
     slots = pl.pallas_call(
         functools.partial(gather_kernel, n),
-        out_shape=jax.ShapeDtypeStruct((n, 1, padded), jnp.float32),
+        out_shape=jax.ShapeDtypeStruct((n * stride,), jnp.float32),
         in_specs=[pl.BlockSpec(memory_space=VMEM)],
         out_specs=pl.BlockSpec(memory_space=VMEM),
         scratch_shapes=[
+            pltpu.VMEM(((piece + LANES - 1) // LANES * LANES,), jnp.float32),
             pltpu.SemaphoreType.DMA((n,)),
             pltpu.SemaphoreType.DMA((n,)),
             pltpu.SemaphoreType.DMA,
         ],
-        compiler_params=pltpu.CompilerParams(collective_id=0, has_side_effects=True),
+        compiler_params=pltpu.CompilerParams(
+            collective_id=0, has_side_effects=True, vmem_limit_bytes=GRANT
+        ),
         name="gather_series",
-    )(row)
+    )(series)
 
     best = pl.pallas_call(
         functools.partial(sweep_kernel, piece, count_len),
@@ -334,8 +344,9 @@
             pltpu.VMEM((TILE_SIDE, MAX_LEN), jnp.bfloat16),
             pltpu.VMEM((MAX_LEN, TILE_SIDE), jnp.bfloat16),
         ],
+        compiler_params=pltpu.CompilerParams(vmem_limit_bytes=32 * GRANT // 2 + points * LANES * 4),
         name="sweep_tiles",
-    )(tile_list, window_lengths, exclusion, slots)
+    )(tile_list.T, window_lengths, exclusion, slots)
 
     block = (2 * count_len, TILE_SIDE)
     profile = jax.ShapeDtypeStruct((len_devices * count_len, TILE_SIDE), jnp.float32)
@@ -354,7 +365,9 @@
             pltpu.SemaphoreType.DMA((len_devices,)),
             pltpu.SemaphoreType.DMA((len_devices,)),
         ],
-        compiler_params=pltpu.CompilerParams(collective_id=1, has_side_effects=True),
+        compiler_params=pltpu.CompilerParams(
+            collective_id=1, has_side_effects=True, vmem_limit_bytes=2 * GRANT
+        ),
         name="exchange_minima",
     )(best)
 

time: 39 us -> 32.9 us (0.84)
  Pallas kernels: 33.3 us -> 29.9 us
  local copies, waits for them, and re-layouts: 4.51 us -> 1.89 us
    pallas_call x1, Pallas kernels: 11.2 us -> 8.62 us  [shards(): pl.pallas_call(functools.partial(sweep_kernel, piece, count_len), out_sha...]
    unnamed x5 -> x10, local copies, waits for them, and re-layouts: 3.24 us -> 1.89 us
    pallas_call x1, Pallas kernels: 10 us -> 8.69 us  [shards(): pl.pallas_call(functools.partial(gather_kernel, n), out_shape=jax.ShapeDt...]
    pad x1 -> x0, local copies, waits for them, and re-layouts: 0.69 us -> none  [shards(): row = jnp.pad(series, (0, padded - piece)).reshape(1, padded)]
    reshape x1 -> x0, local copies, waits for them, and re-layouts: 0.58 us -> none  [shards(): row = jnp.pad(series, (0, padded - piece)).reshape(1, padded)]
    pallas_call x1, Pallas kernels: 12.1 us -> 12.6 us  [shards(): pl.pallas_call(functools.partial(exchange_kernel, len_devices, n), out_sh...]
where the time goes in v3:
time: 32.9 us; the launch traced here: 32.5 us
  Pallas kernels  29.9 us (91%)
  local copies, waits for them, and re-layouts  1.89 us (6%)
  between operations  0.69 us (2%)
    pallas_call x1, Pallas kernels, shards(): pl.pallas_call(functools.partial(exchange_kernel, len_devices, n), out_sh...  12.6 us
    pallas_call x1, Pallas kernels, shards(): pl.pallas_call(functools.partial(gather_kernel, n), out_shape=jax.ShapeDt...  8.69 us
    pallas_call x1, Pallas kernels, shards(): pl.pallas_call(functools.partial(sweep_kernel, piece, count_len), out_sha...  8.62 us
    unnamed x10, local copies, waits for them, and re-layouts  1.89 us

profile of v3, /device:TPU:0, one launch (start us, length us, event | category | flops | bytes accessed | tf_op | source)
XLA Modules:
  0.0 32.5 jit_solution(719249675915765856)
XLA Ops:
  0.6 0.0 copy-start
  0.6 0.7 %copy-done = f32[576]{0:T(1024)S(1)} copy-done((f32[576]{0:T(1024)S(1)}, f32[576]{0:T(1024)}, u32[]{:S(2)}) %copy-start) | copy-done | bytes 2328
  1.3 0.0 copy-start.1
  1.3 0.0 copy-start.2
  1.3 0.0 copy-start.3
  1.3 8.7 %gather_series.1.slots_ref = f32[16384]{0:T(1024)S(1)} custom-call(f32[576]{0:T(1024)S(1)} %copy-done), custom_call_target="tpu_custom_call" | custom-call | tf_op jit(solution)/shard_map/gather_series/pallas_call | solution.py:311
  10.0 0.0 copy-done.1
  10.0 0.0 copy-done.2
  10.0 0.0 copy-done.3
  10.0 8.6 %sweep_tiles.1.best_ref = f32[16,4,512]{2,1,0:T(4,128)S(1)} custom-call(s32[2,4]{1,0:T(2,128)S(1)} %bitcast.1, s32[2]{0:T(128)S(1)} %copy-done.2, s32[2]{0:T(128)S(1)} %copy-done.3, f32[16384]{0:T(1024)S(1)} %gather_series.1.slots_ref), custom_call_target="tpu_custom_call" | custom-call | tf_op jit(solution)/shard_map/sweep_tiles/pallas_call | solution.py:328
  18.7 12.6 %exchange_minima.1 = (f32[4,512]{1,0:T(4,128)S(1)}, f32[4,512]{1,0:T(4,128)S(1)}) custom-call(f32[16,4,512]{2,1,0:T(4,128)S(1)} %sweep_tiles.1.best_ref), custom_call_target="tpu_custom_call" | custom-call | tf_op jit(solution)/shard_map/exchange_minima/pallas_call | solution.py:353
  31.3 0.6 %copy.8 = f32[4,512]{1,0:T(4,128)} copy(f32[4,512]{1,0:T(4,128)S(1)} %get-tuple-element.4) | data formatting | bytes 16384
  31.9 0.6 %copy.9 = f32[4,512]{1,0:T(4,128)} copy(f32[4,512]{1,0:T(4,128)S(1)} %get-tuple-element.5) | data formatting | bytes 16384
Async XLA Ops:
  0.6 0.7 %copy-start = (f32[576]{0:T(1024)S(1)}, f32[576]{0:T(1024)}, u32[]{:S(2)}) copy-start(f32[576]{0:T(1024)} %piece_ref.1) | copy-start | bytes 6916
  1.3 8.7 %copy-start.1 = (s32[4,2]{0,1:T(2,128)S(1)}, s32[4,2]{0,1:T(2,128)}, u32[]{:S(2)}) copy-start(s32[4,2]{0,1:T(2,128)} %param.7) | copy-start | bytes 100
  1.3 8.7 %copy-start.2 = (s32[2]{0:T(128)S(1)}, s32[2]{0:T(128)}, u32[]{:S(2)}) copy-start(s32[2]{0:T(128)} %length_ref.1) | copy-start | bytes 28
  1.3 8.7 %copy-start.3 = (s32[2]{0:T(128)S(1)}, s32[2]{0:T(128)}, u32[]{:S(2)}) copy-start(s32[2]{0:T(128)} %barrier_ref.1) | copy-start | bytes 28

commit v4 on v3

--- a/solution.py
+++ b/solution.py
@@ -1,4 +1,5 @@
 import functools
+import itertools
 
 import jax
 import jax.numpy as jnp
@@ -10,7 +11,6 @@
 MAX_LEN = 1024
 TILE_SIDE = 512
 LANES = 128
-CHUNK = 256
 GRANT = 1 << 20
 FLAT = 1024
 
@@ -215,57 +215,40 @@
     best_ref[...] = jnp.full(best_ref.shape, EMPTY_VALUE, jnp.float32)
     quarters = TILE_SIDE // LANES
 
-    def one_product(index, carry):
-        slot, l = index // count_len, lax.rem(index, count_len)
+    def one_product(slot, l, depth):
         row_block, col_block = tile_ref[0, slot], tile_ref[1, slot]
         length, barrier = length_ref[l], barrier_ref[l]
         size = length.astype(jnp.float32)
-        chunks = (length + CHUNK - 1) // CHUNK
         row_first, col_first = row_block * quarters, col_block * quarters
         limit = barrier - (col_block - row_block) * TILE_SIDE
 
         def finish(depth):
-            turned = jnp.transpose(
+            row_centre, row_inverse, col_centre, col_inverse = (
                 jnp.concatenate(
-                    [
-                        centre_ref[l, pl.ds(row_first, quarters), :],
-                        inverse_ref[l, pl.ds(row_first, quarters), :],
-                    ],
-                    axis=0,
+                    [source[l, pl.ds(start + u, 1), :] for u in range(quarters)], axis=1
                 )
-            )
-            col_centre, col_inverse = (
-                jnp.concatenate(
-                    [source[l, pl.ds(col_first + u, 1), :] for u in range(quarters)], axis=1
-                )
+                for start in (row_first, col_first)
                 for source in (centre_ref, inverse_ref)
             )
             for k in range(depth // LANES):
                 spot = pl.ds(pl.multiple_of((col_first + k) * LANES, LANES), TILE_SIDE)
-                right_op[k * LANES : (k + 1) * LANES, :] = (
+                right_op[l, k * LANES : (k + 1) * LANES, :] = (
                     (base[:, spot] - col_centre) * col_inverse
                 ).astype(jnp.bfloat16)
-            sure = depth - CHUNK
-            lane_ids = lax.broadcasted_iota(jnp.int32, (16, CHUNK), 1)
-            inside = lane_ids < length - sure
+            for k in range(depth // LANES):
+                inside = lax.broadcasted_iota(jnp.int32, (LANES, TILE_SIDE), 0) < length - k * LANES
+                spot = pl.ds(pl.multiple_of((row_first + k) * LANES, LANES), TILE_SIDE)
+                left_op[l, k * LANES : (k + 1) * LANES, :] = jnp.where(
+                    inside, (base[:, spot] - row_centre) * row_inverse, 0.0
+                ).astype(jnp.bfloat16)
             col_best = None
             row_best = []
             for half in range(0, quarters, 2):
-                for q in range(half, half + 2):
-                    spot = pl.ds(pl.multiple_of((row_first + q) * LANES, LANES), depth)
-                    for g in range(0, LANES, 16):
-                        values = (base[g : g + 16, spot] - turned[g : g + 16, q : q + 1]) * turned[
-                            g : g + 16, quarters + q : quarters + q + 1
-                        ]
-                        last = jnp.where(inside, values[:, sure:], 0.0)
-                        at = q * LANES + g
-                        if sure:
-                            left_op[at : at + 16, :sure] = values[:, :sure].astype(jnp.bfloat16)
-                        left_op[at : at + 16, sure:depth] = last.astype(jnp.bfloat16)
                 low = half * LANES
-                product = jnp.dot(
-                    left_op[low : low + 2 * LANES, :depth],
-                    right_op[:depth, :],
+                product = lax.dot_general(
+                    left_op[l, :depth, low : low + 2 * LANES],
+                    right_op[l, :depth, :],
+                    (((0,), (0,)), ((), ())),
                     preferred_element_type=jnp.float32,
                 )
                 ahead = lax.broadcasted_iota(jnp.int32, product.shape, 1) - (
@@ -286,15 +269,23 @@
             spot = (col_block, pl.ds(count_len + l, 1))
             best_ref[spot] = jnp.minimum(best_ref[spot], 1.0 - col_best / size)
 
-        for count in range(1, MAX_LEN // CHUNK + 1):
-
-            @pl.when(chunks == count)
+        finish(depth)
+
+    def one_slot(slot, carry):
+        for depths in itertools.product((MAX_LEN // 2, MAX_LEN), repeat=count_len):
+            fits = [
+                jnp.logical_and(length_ref[l] <= depth, length_ref[l] > depth - MAX_LEN // 2)
+                for l, depth in enumerate(depths)
+            ]
+
+            @pl.when(functools.reduce(jnp.logical_and, fits))
             def _():
-                finish(count * CHUNK)
+                for l, depth in enumerate(depths):
+                    one_product(slot, l, depth)
 
         return carry
 
-    lax.fori_loop(0, tile_ref.shape[1] * count_len, one_product, 0)
+    lax.fori_loop(0, tile_ref.shape[1], one_slot, 0)
 
 
 def shards(series, window_lengths, exclusion, tile_list):
@@ -341,8 +332,8 @@
             pltpu.VMEM((columns, LANES), jnp.float32),
             pltpu.VMEM((count_len, columns, LANES), jnp.float32),
             pltpu.VMEM((count_len, columns, LANES), jnp.float32),
-            pltpu.VMEM((TILE_SIDE, MAX_LEN), jnp.bfloat16),
-            pltpu.VMEM((MAX_LEN, TILE_SIDE), jnp.bfloat16),
+            pltpu.VMEM((count_len, MAX_LEN, TILE_SIDE), jnp.bfloat16),
+            pltpu.VMEM((count_len, MAX_LEN, TILE_SIDE), jnp.bfloat16),
         ],
         compiler_params=pltpu.CompilerParams(vmem_limit_bytes=32 * GRANT // 2 + points * LANES * 4),
         name="sweep_tiles",

time: 32.9 us -> 32 us (0.973)
  Pallas kernels: 29.9 us -> 28.9 us
    pallas_call x1, Pallas kernels: 12.6 us -> 10.9 us  [shards(): pl.pallas_call(functools.partial(exchange_kernel, len_devices, n), out_sh...]
    pallas_call x1, Pallas kernels: 8.62 us -> 9.33 us  [shards(): pl.pallas_call(functools.partial(sweep_kernel, piece, count_len), out_sha...]
where the time goes in v4:
time: 32 us; the launch traced here: 31.5 us
  Pallas kernels  28.9 us (90%)
  local copies, waits for them, and re-layouts  1.89 us (6%)
  between operations  0.69 us (2%)
    pallas_call x1, Pallas kernels, shards(): pl.pallas_call(functools.partial(exchange_kernel, len_devices, n), out_sh...  10.9 us
    pallas_call x1, Pallas kernels, shards(): pl.pallas_call(functools.partial(sweep_kernel, piece, count_len), out_sha...  9.33 us
    pallas_call x1, Pallas kernels, shards(): pl.pallas_call(functools.partial(gather_kernel, n), out_shape=jax.ShapeDt...  8.69 us
    unnamed x10, local copies, waits for them, and re-layouts  1.89 us

profile of v4, /device:TPU:0, one launch (start us, length us, event | category | flops | bytes accessed | tf_op | source)
XLA Modules:
  0.0 31.5 jit_solution(2179917328878288217)
XLA Ops:
  0.6 0.0 copy-start
  0.6 0.7 %copy-done = f32[576]{0:T(1024)S(1)} copy-done((f32[576]{0:T(1024)S(1)}, f32[576]{0:T(1024)}, u32[]{:S(2)}) %copy-start) | copy-done | bytes 2328
  1.3 0.0 copy-start.1
  1.3 0.0 copy-start.2
  1.3 0.0 copy-start.3
  1.3 8.7 %gather_series.1.slots_ref = f32[16384]{0:T(1024)S(1)} custom-call(f32[576]{0:T(1024)S(1)} %copy-done), custom_call_target="tpu_custom_call" | custom-call | tf_op jit(solution)/shard_map/gather_series/pallas_call | solution.py:302
  10.0 0.0 copy-done.1
  10.0 0.0 copy-done.2
  10.0 0.0 copy-done.3
  10.0 9.3 %sweep_tiles.1.best_ref = f32[16,4,512]{2,1,0:T(4,128)S(1)} custom-call(s32[2,4]{1,0:T(2,128)S(1)} %bitcast.1, s32[2]{0:T(128)S(1)} %copy-done.2, s32[2]{0:T(128)S(1)} %copy-done.3, f32[16384]{0:T(1024)S(1)} %gather_series.1.slots_ref), custom_call_target="tpu_custom_call" | custom-call | tf_op jit(solution)/shard_map/sweep_tiles/pallas_call | solution.py:319
  19.4 10.9 %exchange_minima.1 = (f32[4,512]{1,0:T(4,128)S(1)}, f32[4,512]{1,0:T(4,128)S(1)}) custom-call(f32[16,4,512]{2,1,0:T(4,128)S(1)} %sweep_tiles.1.best_ref), custom_call_target="tpu_custom_call" | custom-call | tf_op jit(solution)/shard_map/exchange_minima/pallas_call | solution.py:344
  30.3 0.6 %copy.8 = f32[4,512]{1,0:T(4,128)} copy(f32[4,512]{1,0:T(4,128)S(1)} %get-tuple-element.4) | data formatting | bytes 16384
  30.9 0.6 %copy.9 = f32[4,512]{1,0:T(4,128)} copy(f32[4,512]{1,0:T(4,128)S(1)} %get-tuple-element.5) | data formatting | bytes 16384
Async XLA Ops:
  0.6 0.7 %copy-start = (f32[576]{0:T(1024)S(1)}, f32[576]{0:T(1024)}, u32[]{:S(2)}) copy-start(f32[576]{0:T(1024)} %piece_ref.1) | copy-start | bytes 6916
  1.3 8.7 %copy-start.1 = (s32[4,2]{0,1:T(2,128)S(1)}, s32[4,2]{0,1:T(2,128)}, u32[]{:S(2)}) copy-start(s32[4,2]{0,1:T(2,128)} %param.7) | copy-start | bytes 100
  1.3 8.7 %copy-start.2 = (s32[2]{0:T(128)S(1)}, s32[2]{0:T(128)}, u32[]{:S(2)}) copy-start(s32[2]{0:T(128)} %length_ref.1) | copy-start | bytes 28
  1.3 8.7 %copy-start.3 = (s32[2]{0:T(128)S(1)}, s32[2]{0:T(128)}, u32[]{:S(2)}) copy-start(s32[2]{0:T(128)} %barrier_ref.1) | copy-start | bytes 28
